TPU v7x, 512 devices: a whole 4x8x8 slice. The times are simulated.
512 devices in a mesh: ex: 32 (over x, z), feat: 16 (over y, core).
Axes of the slice: x: 4, y: 8, z: 8, core: 2. Of those that a mesh axis runs over, the one named last changes fastest.
Arguments:
- pooled: bfloat16 [65536, 8192], P('ex', 'feat'), may hold values from -6 to 6
- labels: int32 [65536], P('ex'), may hold values from 0 to 1
- sign_bits: int32 [65536], P('ex'), may hold values from 0 to 1
- margins_old: float32 [65536], P('ex'), may hold values from -8 to 8
- direction: float32 [8192], P(('feat', 'ex')), may hold values from -0.0625 to 0.0625
- sample_rows: int32 [1024], replicated, may hold values from 0 to 65535
Outputs:
- margins: float32 [65536], P('ex')
- gradient: float32 [8192], P(('feat', 'ex'))
- sketch: float32 [1024, 8192], P('ex', 'feat')
Inputs may be any that keep to these rules, and one draw needn't show every extreme that they name: `sample_rows`: indices are drawn independently, repeats possible.
All inputs are finite; a program needn't handle non-finite values.
Results may differ from a plain program's by a relative error of at most 0.0033.
Values may be sent and summed in bfloat16 or wider, within the bound.
A program may use at most 64 MiB of HBM per device.

v0:
```python
import math

import jax
import jax.numpy as jnp
from jax import lax
from jax.sharding import PartitionSpec as P


def joined_along(blocks, dim):
    blocks = jnp.moveaxis(blocks, 0, dim)
    shape = blocks.shape
    return blocks.reshape(*shape[:dim], shape[dim] * shape[dim + 1], *shape[dim + 2 :])


def copy_for_each(x, axis):
    count = lax.axis_size(axis)
    return lax.all_to_all(jnp.broadcast_to(x[None], (count, *x.shape)), axis, 0, 0, tiled=True)


def gather_directly(x, axis, dim):
    return joined_along(copy_for_each(x, axis), dim)


def of_everyone(x, axis):
    return copy_for_each(x, axis).sum(axis=0)


def in_blocks(x, dim, count):
    shape = x.shape
    blocks = x.reshape(*shape[:dim], count, shape[dim] // count, *shape[dim + 1 :])
    return jnp.moveaxis(blocks, dim, 0)


def summed_on_arrival(x, axis, dim):
    count = lax.axis_size(axis)
    blocks = lax.all_to_all(in_blocks(x, dim, count), axis, 0, 0, tiled=True)
    return jnp.sum(blocks, axis=0)


def parity_table(row_ids, col_ids):
    folded = jnp.bitwise_and(row_ids[:, None], col_ids[None, :])
    for shift_by in (16, 8, 4, 2, 1):
        folded = jnp.bitwise_xor(folded, jnp.right_shift(folded, shift_by))
    odd_bit = jnp.bitwise_and(folded, 1)
    return (1 - 2 * odd_bit).astype(jnp.bfloat16)


def response(margins, labels):
    residual = jax.nn.sigmoid(margins) - labels.astype(jnp.float32)
    weight = jnp.sqrt(jax.nn.sigmoid(margins) * jax.nn.sigmoid(-margins))
    return (residual, weight)


def on_device(pooled, labels, sign_bits, margins_old, direction, sample_rows):
    row_count = pooled.shape[0]
    ex_count = lax.axis_size("ex")
    total_rows = row_count * ex_count
    ex_index = lax.axis_index("ex")
    pieces = gather_directly(direction.astype(jnp.bfloat16), "ex", 0)
    partial_margins = jnp.dot(pooled, pieces, preferred_element_type=jnp.float32)
    margins = margins_old + of_everyone(partial_margins, "feat")
    residual, weight = response(margins, labels)
    residual_b = residual.astype(jnp.bfloat16)
    gradient = summed_on_arrival(
        jnp.dot(residual_b, pooled, preferred_element_type=jnp.float32), "ex", 0
    ) / math.sqrt(total_rows)
    scale_rows = (2 * sign_bits - 1).astype(jnp.float32) * weight
    weighted = (pooled * scale_rows[:, None]).astype(jnp.bfloat16)
    sketch_count = sample_rows.shape[0]
    col_ids = ex_index * row_count + jnp.arange(row_count, dtype=jnp.int32)
    signs_table = parity_table(sample_rows, col_ids)
    sketch = summed_on_arrival(
        jnp.dot(signs_table, weighted, preferred_element_type=jnp.float32), "ex", 0
    ) / math.sqrt(sketch_count)
    return (margins, gradient, sketch)


def solution(mesh):
    return jax.shard_map(
        on_device,
        mesh=mesh,
        in_specs=(P("ex", "feat"), P("ex"), P("ex"), P("ex"), P(("feat", "ex")), P()),
        out_specs=(P("ex"), P(("feat", "ex")), P("ex", "feat")),
        check_vma=False,
    )
```

profile of v0, /device:TPU:1, one launch (start us, length us, event | category | flops | bytes accessed | tf_op | source)
XLA Modules:
  0.0 115.1 jit_solution(9333846103416625223)
XLA Ops:
  0.6 0.0 copy-start
  0.6 0.0 copy-start.3
  0.7 0.0 copy-start.2
  0.7 0.0 copy-start.4
  0.7 0.8 convert_element_type.21
  1.5 22.2 %all_to_all.26 = bf16[32,1,16]{2,1,0:T(2,128)(2,1)S(1)} all-to-all(bf16[32,1,16]{2,1,0:T(2,128)(2,1)S(1)} %broadcast_in_dim.4), channel_id=1, replica_groups=mesh['ex'=32,'feat'=16] {'ex'}, dimensions={0} | all-to-all | bytes 2048 | tf_op jit(solution)/shard_map/all_to_all | solution.py:17
  23.7 0.1 reduce.2
  23.7 0.1 reshape.37
  23.8 0.0 copy-start.5
  23.8 2.2 %fusion.19 = f32[1,2048]{1,0:T(1,128)S(1)} fusion(bf16[2048,512]{1,0:T(8,128)(2,1)} %param.6, bf16[512,1]{0,1:T(2,128)(2,1)S(1)} %reshape.37), kind=kOutput, calls=%fused_computation.30 | convolution fusion | flops 2097152 | bytes 2106368 | tf_op jit(solution)/shard_map/dot_general | solution.py:60
  26.1 0.7 broadcast_in_dim.5
  26.8 9.2 %all-to-all-start.1 = ((f32[16,1,2048]{2,1,0:T(1,128)}), f32[16,1,2048]{2,1,0:T(1,128)S(1)}, u32[]{:S(2)}, u32[]{:S(2)}) async-start(f32[16,1,2048]{2,1,0:T(1,128)} %broadcast_in_dim.5), calls=%async_computation.1 | async-start | bytes 262144 | tf_op jit(solution)/shard_map/all_to_all | solution.py:17
  36.0 8.9 %all-to-all-done.1 = f32[16,1,2048]{2,1,0:T(1,128)S(1)} async-done(((f32[16,1,2048]{2,1,0:T(1,128)}), f32[16,1,2048]{2,1,0:T(1,128)S(1)}, u32[]{:S(2)}, u32[]{:S(2)}) %all-to-all-start.1) | async-done | bytes 131104 | tf_op jit(solution)/shard_map/all_to_all | solution.py:17
  44.9 0.1 reduce_sum.27
  45.0 0.0 copy-done.3
  45.0 0.0 copy-done.2
  45.0 0.0 copy-start.1
  45.0 0.0 copy-done.4
  45.1 0.0 copy-done
  45.1 0.4 fusion.20
  45.5 0.7 all_to_all.19
  46.2 3.8 %all-to-all-start.2 = ((f32[32,1,16]{2,1,0:T(1,128)}), f32[32,1,16]{2,1,0:T(1,128)S(1)}, u32[]{:S(2)}, u32[]{:S(2)}) async-start(f32[32,1,16]{2,1,0:T(1,128)} %bitcast.2), calls=%async_computation.2 | async-start | bytes 32768 | tf_op jit(solution)/shard_map/all_to_all | solution.py:36
  50.0 0.0 copy-done.5
  50.0 6.1 %fusion.4 = f32[1024,512]{1,0:T(8,128)} fusion(s32[2048]{0:T(1024)S(1)} %iota_add_fusion, s32[1024]{0:T(1024)S(1)} %copy-done.5, bf16[2048,512]{1,0:T(8,128)(2,1)S(1)} %copy-done, f32[2048]{0:T(1024)S(1)} %get-tuple-element.3), kind=kOutput, calls=%fused_computation.9 | convolution fusion | flops 2182086656 | bytes 4214784 | tf_op jit(solution)/shard_map/dot_general | solution.py:73
  56.1 0.0 copy-done.1
  56.1 2.4 %all-to-all-done.2 = f32[32,1,16]{2,1,0:T(1,128)S(1)} async-done(((f32[32,1,16]{2,1,0:T(1,128)}), f32[32,1,16]{2,1,0:T(1,128)S(1)}, u32[]{:S(2)}, u32[]{:S(2)}) %all-to-all-start.2) | async-done | bytes 2080 | tf_op jit(solution)/shard_map/all_to_all | solution.py:36
  58.6 6.8 %all-to-all-start.3 = ((f32[32,32,512]{2,1,0:T(8,128)}), f32[32,32,512]{2,1,0:T(8,128)S(1)}, u32[]{:S(2)}, u32[]{:S(2)}) async-start(f32[32,32,512]{2,1,0:T(8,128)} %bitcast.8), calls=%async_computation.3 | async-start | bytes 4194304 | tf_op jit(solution)/shard_map/all_to_all | solution.py:36
  65.4 0.1 reduce_sum.28
  65.4 0.5 broadcast_multiply_fusion.1
  66.0 48.4 %all-to-all-done.3 = f32[32,32,512]{2,1,0:T(8,128)S(1)} async-done(((f32[32,32,512]{2,1,0:T(8,128)}), f32[32,32,512]{2,1,0:T(8,128)S(1)}, u32[]{:S(2)}, u32[]{:S(2)}) %all-to-all-start.3) | async-done | bytes 2097184 | tf_op jit(solution)/shard_map/all_to_all | solution.py:36
  114.3 0.1 reduce_sum.29
  114.5 0.6 broadcast_multiply_fusion
  (5 shorter events, 0.1 us)
Async XLA Ops:
  0.6 44.4 %copy-start = (bf16[2048,512]{1,0:T(8,128)(2,1)S(1)}, bf16[2048,512]{1,0:T(8,128)(2,1)}, u32[]{:S(2)}) copy-start(bf16[2048,512]{1,0:T(8,128)(2,1)} %param.6) | copy-start | bytes 6291460
  0.6 44.3 %copy-start.3 = (f32[2048]{0:T(1024)S(1)}, f32[2048]{0:T(1024)}, u32[]{:S(2)}) copy-start(f32[2048]{0:T(1024)} %param.9) | copy-start | bytes 24580
  0.7 44.3 %copy-start.2 = (s32[2048]{0:T(1024)S(1)}, s32[2048]{0:T(1024)}, u32[]{:S(2)}) copy-start(s32[2048]{0:T(1024)} %param.8) | copy-start | bytes 24580
  0.7 44.4 %copy-start.4 = (s32[2048]{0:T(1024)S(1)}, s32[2048]{0:T(1024)}, u32[]{:S(2)}) copy-start(s32[2048]{0:T(1024)} %param.7) | copy-start | bytes 24580
  23.8 26.2 %copy-start.5 = (s32[1024]{0:T(1024)S(1)}, s32[1024]{0:T(1024)}, u32[]{:S(2)}) copy-start(s32[1024]{0:T(1024)} %param.11) | copy-start | bytes 12292
  26.8 18.1 %all-to-all-start.1 = ((f32[16,1,2048]{2,1,0:T(1,128)}), f32[16,1,2048]{2,1,0:T(1,128)S(1)}, u32[]{:S(2)}, u32[]{:S(2)}) async-start(f32[16,1,2048]{2,1,0:T(1,128)} %broadcast_in_dim.5), calls=%async_computation.1 | async-start | bytes 262144 | tf_op jit(solution)/shard_map/all_to_all | solution.py:17
  45.0 11.1 %copy-start.1 = (f32[2048]{0:T(1024)}, f32[2048]{0:T(1024)S(1)}, u32[]{:S(2)}) copy-start(f32[2048]{0:T(1024)S(1)} %get-tuple-element.4) | copy-start | bytes 24580
  46.2 12.4 %all-to-all-start.2 = ((f32[32,1,16]{2,1,0:T(1,128)}), f32[32,1,16]{2,1,0:T(1,128)S(1)}, u32[]{:S(2)}, u32[]{:S(2)}) async-start(f32[32,1,16]{2,1,0:T(1,128)} %bitcast.2), calls=%async_computation.2 | async-start | bytes 32768 | tf_op jit(solution)/shard_map/all_to_all | solution.py:36
  58.6 55.7 %all-to-all-start.3 = ((f32[32,32,512]{2,1,0:T(8,128)}), f32[32,32,512]{2,1,0:T(8,128)S(1)}, u32[]{:S(2)}, u32[]{:S(2)}) async-start(f32[32,32,512]{2,1,0:T(8,128)} %bitcast.8), calls=%async_computation.3 | async-start | bytes 4194304 | tf_op jit(solution)/shard_map/all_to_all | solution.py:36
where the time goes:
time: 115 us
  waiting for transfers between devices  59.7 us (52%)
  blocking collectives  22.2 us (19%)
  starting transfers between devices  19.8 us (17%)
  matrix products  8.75 us (8%)
  other arithmetic  2.32 us (2%)
  local copies, waits for them, and re-layouts  1.56 us (1%)
    all_to_all x2, waiting for transfers between devices, summed_on_arrival(): blocks = lax.all_to_all(in_blocks(x, dim, count), axis, 0, 0, tiled=True)  50.8 us
    all_to_all x1, blocking collectives, copy_for_each(): lax.all_to_all(jnp.broadcast_to(x[None], (count, *x.shape)), axis, 0, 0,...  22.2 us
    all_to_all x2, starting transfers between devices, summed_on_arrival(): blocks = lax.all_to_all(in_blocks(x, dim, count), axis, 0, 0, tiled=True)  10.6 us
    all_to_all x1, starting transfers between devices, copy_for_each(): lax.all_to_all(jnp.broadcast_to(x[None], (count, *x.shape)), axis, 0, 0,...  9.22 us
    all_to_all x1, waiting for transfers between devices, copy_for_each(): lax.all_to_all(jnp.broadcast_to(x[None], (count, *x.shape)), axis, 0, 0,...  8.88 us
    dot_general x1, matrix products, on_device(): jnp.dot(signs_table, weighted, preferred_element_type=jnp.float32)  6.14 us
  transfers between devices with their start and end apart: 3, of which 3 were waited for; matrix products, arithmetic and copies ran while one was open for 6% of the time, Pallas kernels for 0%

commit v1 on v0

v1 whole, which is shorter than its diff:
```python
import jax
import jax.numpy as jnp
from jax import lax
from jax.experimental import pallas as pl
from jax.experimental.pallas import tpu as pltpu
from jax.sharding import PartitionSpec as P

NX, NZ, NF = 4, 8, 16
ROWS, COLS, SAMPLES, LANES = 2048, 512, 1024, 128
HALF = COLS // 2
BLOCKS = ROWS // LANES
OWNED = SAMPLES // (NX * NZ)
OFFSETS = (4, 3, 5, 2, 6, 1, 7, 0)
F32, BF16 = jnp.float32, jnp.bfloat16
MESH = pl.DeviceIdType.MESH


def parity_sign(ids, mask):
    return 1 - 2 * jnp.bitwise_and(lax.population_count(jnp.bitwise_and(ids, mask)), 1)


def kernel(
    pooled_hbm, labels_hbm, bits_hbm, old_hbm, dir_hbm, rows_hbm,
    margins_out, grad_out, sketch_out,
    pooled, labels, bits, old, own_dir, rows,
    ids, table, weighted, zdir, xdir, terms,
    xgrad_send, xgrad, zgrad_send, zgrad,
    keep_a, keep_b, send_a, send_b, got_a, got_b,
    second_a, second_b, last_a, last_b, zsend, zgot,
    in_sem, zdir_sem, xdir_sem, terms_sem, xgrad_sem, zgrad_sem,
    first_sem, second_sem, zsketch_sem,
):
    ex = lax.axis_index("ex")
    feat = lax.axis_index("feat")
    x, z = ex // NZ, ex % NZ
    flip = x + 1 - 2 * (x % 2)
    back = NX - 1 - x
    across = (x + 2) % NX
    groups = (x, flip, back, across)

    def at_x(other):
        return {"ex": other * NZ + z}

    def at_z(step):
        return {"ex": x * NZ + (z + step) % NZ}

    def at_feat(step):
        return {"feat": (feat + step) % NF}

    loads = [
        pltpu.make_async_copy(src, dst, in_sem.at[i])
        for i, (src, dst) in enumerate(
            ((dir_hbm, own_dir), (rows_hbm, rows), (pooled_hbm, pooled), (old_hbm, old), (labels_hbm, labels), (bits_hbm, bits))
        )
    ]
    for load in loads:
        load.start()

    barrier = pltpu.get_barrier_semaphore()
    for step in range(1, NX):
        pl.semaphore_signal(barrier, inc=1, device_id=at_x((x + step) % NX), device_id_type=MESH)
    for step in range(1, NZ):
        pl.semaphore_signal(barrier, inc=1, device_id=at_z(step), device_id_type=MESH)
    for step in range(1, NF):
        pl.semaphore_signal(barrier, inc=1, device_id=at_feat(step), device_id_type=MESH)

    def remote(src, dst, sems, slot, device):
        return pltpu.make_async_remote_copy(
            src_ref=src, dst_ref=dst, send_sem=sems.at[0, slot], recv_sem=sems.at[1, slot], device_id=device, device_id_type=MESH
        )

    loads[0].wait()
    lane_row = lax.broadcasted_iota(jnp.int32, (1, LANES), 1)
    spread = jnp.concatenate([own_dir[...]] * NZ, axis=1)
    zdir[0] = jnp.where(lane_row // 16 == z, spread, 0.0)

    loads[1].wait()
    turned = jnp.transpose(rows[...])
    for t in range(SAMPLES // LANES):
        ids[t * LANES : (t + 1) * LANES, :] = jnp.broadcast_to(turned[:, t : t + 1], (LANES, LANES))

    def table_block(index):
        part, step = index // NZ, index % NZ
        offset = jnp.where(step % 2 == 0, NZ // 2 + step // 2, NZ // 2 - (step + 1) // 2)
        owner = jnp.where(part == 0, x, jnp.where(part == 1, flip, jnp.where(part == 2, back, across)))
        start = pl.multiple_of(owner * (NZ * OWNED) + (z + offset) % NZ * OWNED, OWNED)
        there = pl.multiple_of(step * (NX * OWNED) + part * OWNED, OWNED)
        wanted = ids[pl.ds(start, OWNED), :]
        lanes = lax.broadcasted_iota(jnp.int32, (OWNED, LANES), 1)
        signs = [None] * BLOCKS
        signs[0] = parity_sign(wanted, ex * ROWS + lanes).astype(F32).astype(BF16)
        for bit in range(4):
            this = (1 - 2 * jnp.bitwise_and(jnp.right_shift(wanted, 7 + bit), 1)).astype(F32).astype(BF16)
            for low in range(1 << bit):
                signs[low + (1 << bit)] = signs[low] * this
        for block in range(BLOCKS):
            table[pl.ds(there, OWNED), block * LANES : (block + 1) * LANES] = signs[block]

    pl.loop(0, 8)(table_block)
    pl.semaphore_wait(barrier, NX + NZ + NF - 3)

    zdir_copies = [remote(zdir.at[0], zdir.at[step], zdir_sem, step, at_z(step)) for step in range(1, NZ)]
    for copy in zdir_copies:
        copy.start()
    pl.loop(8, 24)(table_block)
    for copy in zdir_copies:
        copy.wait_recv()
    row = zdir[0]
    for step in range(1, NZ):
        row = row + zdir[step]
    xdir[x] = row
    xdir_copies = [remote(xdir.at[x], xdir.at[x], xdir_sem, step, at_x((x + step) % NX)) for step in range(1, NX)]
    for copy in xdir_copies:
        copy.start()
    pl.loop(24, 32)(table_block)
    loads[2].wait()
    for copy in xdir_copies:
        copy.wait_recv()

    step_dir = jnp.concatenate([xdir[i] for i in range(NX)], axis=1).astype(BF16)
    step_dir = jnp.broadcast_to(step_dir, (BLOCKS, COLS))
    block_row = lax.broadcasted_iota(jnp.int32, (BLOCKS, LANES), 0)
    partial = jnp.zeros((BLOCKS, LANES), F32)
    for block in range(BLOCKS):
        here = lax.dot_general(
            step_dir,
            pooled[block * LANES : (block + 1) * LANES, :],
            (((1,), (1,)), ((), ())),
            preferred_element_type=F32,
        )
        partial = jnp.where(block_row == block, here, partial)
    terms[feat] = partial.astype(BF16)
    terms_copies = [remote(terms.at[feat], terms.at[feat], terms_sem, step, at_feat(step)) for step in range(1, NF)]
    for copy in terms_copies:
        copy.start()
    for load in loads[3:]:
        load.wait()
    for copy in terms_copies:
        copy.wait_recv()
    total = terms[0].astype(F32)
    for i in range(1, NF):
        total = total + terms[i].astype(F32)
    margins = old[...] + total
    margins_out[...] = margins
    decay = jnp.exp(-jnp.abs(margins))
    likely = 1.0 / (1.0 + decay)
    rare = decay * likely
    weight = jnp.sqrt(likely * rare)
    residual = jnp.where(margins >= 0, likely, rare) - labels[...].astype(F32)
    scale = (2 * bits[...] - 1).astype(F32) * weight
    columns = jnp.transpose(scale)
    for block in range(BLOCKS):
        at = slice(block * LANES, (block + 1) * LANES)
        weighted[at, :] = (pooled[at, :].astype(F32) * columns[:, block : block + 1]).astype(BF16)

    def compute(pair):
        at = slice(pair * 2 * NX * OWNED, (pair + 1) * 2 * NX * OWNED)
        left = jnp.dot(table[at, :], weighted[:, :HALF], preferred_element_type=F32)
        right = jnp.dot(table[at, :], weighted[:, HALF:], preferred_element_type=F32)
        for k in range(2):
            c = 2 * pair + k
            g = [slice((k * NX + i) * OWNED, (k * NX + i + 1) * OWNED) for i in range(NX)]
            keep_a[c, :OWNED, :] = left[g[0]]
            keep_a[c, OWNED:, :] = left[g[2]]
            send_a[c, :OWNED, :] = left[g[1]].astype(BF16)
            send_a[c, OWNED:, :] = left[g[3]].astype(BF16)
            keep_b[c] = right[g[0].start : g[1].stop]
            send_b[c] = right[g[2].start : g[3].stop].astype(BF16)

    pending = []

    def launch(*copies):
        for copy in copies:
            copy.start()
            pending.append(copy)
        return copies

    def first(c):
        return launch(
            remote(send_a.at[c], got_a.at[c], first_sem, 2 * c, at_x(flip)),
            remote(send_b.at[c], got_b.at[c], first_sem, 2 * c + 1, at_x(back)),
        )

    def second(c, copies):
        for copy in copies:
            copy.wait_recv()
        second_a[c] = (keep_a[c, OWNED:, :] + got_a[c, OWNED:, :].astype(F32)).astype(BF16)
        second_b[c] = (keep_b[c, OWNED:, :] + got_b[c, OWNED:, :].astype(F32)).astype(BF16)
        return launch(
            remote(second_a.at[c], last_a.at[c], second_sem, 2 * c, at_x(back)),
            remote(second_b.at[c], last_b.at[c], second_sem, 2 * c + 1, at_x(flip)),
        )

    def third(c, copies):
        for copy in copies:
            copy.wait_recv()
        sum_a = keep_a[c, :OWNED, :] + got_a[c, :OWNED, :].astype(F32) + last_a[c].astype(F32)
        sum_b = keep_b[c, :OWNED, :] + got_b[c, :OWNED, :].astype(F32) + last_b[c].astype(F32)
        if OFFSETS[c] == 0:
            return sum_a, sum_b
        zsend[c, :, :HALF] = sum_a.astype(BF16)
        zsend[c, :, HALF:] = sum_b.astype(BF16)
        return launch(remote(zsend.at[c], zgot.at[c], zsketch_sem, c, at_z(OFFSETS[c])))

    ones, twos, threes = {}, {}, {}
    compute(0)
    ones[0], ones[1] = first(0), first(1)
    compute(1)
    ones[2], ones[3] = first(2), first(3)

    flat = jnp.concatenate([residual[i : i + 1, :] for i in range(BLOCKS)], axis=1).astype(BF16)
    grad = jnp.dot(jnp.broadcast_to(flat, (8, ROWS)), pooled[...], preferred_element_type=F32)[0:1, :]
    for i in range(NX):
        xgrad_send[i] = grad[:, i * LANES : (i + 1) * LANES]
    xgrad_copies = launch(*(
        remote(xgrad_send.at[(x + step) % NX], xgrad.at[step], xgrad_sem, step, at_x((x + step) % NX)) for step in range(1, NX)
    ))

    compute(2)
    compute(3)
    for c in range(NZ):
        twos[c] = second(c, ones[c])
        if c + 4 < NZ:
            ones[c + 4] = first(c + 4)
        if c == 1:
            for copy in xgrad_copies:
                copy.wait_recv()
            part = xgrad_send[x]
            for step in range(1, NX):
                part = part + xgrad[step]
            zgrad_send[...] = part
            zgrad_copies = launch(*(remote(zgrad_send, zgrad.at[step], zgrad_sem, step, at_z(step)) for step in range(1, NZ)))
        if c >= 2:
            threes[c - 2] = third(c - 2, twos[c - 2])
    threes[NZ - 2] = third(NZ - 2, twos[NZ - 2])

    for copy in zgrad_copies:
        copy.wait_recv()
    part = zgrad_send[...]
    for step in range(1, NZ):
        part = part + zgrad[step]
    grad_out[...] = pltpu.roll(part, (NZ - z) * 16 % LANES, 1) * (1.0 / 256.0)

    sum_a, sum_b = third(NZ - 1, twos[NZ - 1])
    for c in range(NZ - 1):
        threes[c][0].wait_recv()
        sum_a = sum_a + zgot[c, :, :HALF].astype(F32)
        sum_b = sum_b + zgot[c, :, HALF:].astype(F32)
    sketch_out[:, :HALF] = sum_a * (1.0 / 32.0)
    sketch_out[:, HALF:] = sum_b * (1.0 / 32.0)

    for copy in (*zdir_copies, *xdir_copies, *terms_copies, *pending):
        copy.wait_send()


def on_device(pooled, labels, sign_bits, margins_old, direction, sample_rows):
    dma = pltpu.SemaphoreType.DMA
    vmem = pltpu.VMEM
    margins, grad, sketch = pl.pallas_call(
        kernel,
        out_shape=(
            jax.ShapeDtypeStruct((BLOCKS, LANES), F32),
            jax.ShapeDtypeStruct((1, LANES), F32),
            jax.ShapeDtypeStruct((OWNED, COLS), F32),
        ),
        in_specs=[pl.BlockSpec(memory_space=pl.ANY)] * 6,
        out_specs=[pl.BlockSpec(memory_space=vmem)] * 3,
        scratch_shapes=[
            vmem((ROWS, COLS), BF16),
            vmem((BLOCKS, LANES), jnp.int32),
            vmem((BLOCKS, LANES), jnp.int32),
            vmem((BLOCKS, LANES), F32),
            vmem((1, 16), F32),
            vmem((SAMPLES // LANES, LANES), jnp.int32),
            vmem((SAMPLES, LANES), jnp.int32),
            vmem((SAMPLES, ROWS), BF16),
            vmem((ROWS, COLS), BF16),
            vmem((NZ, 1, LANES), F32),
            vmem((NX, 1, LANES), F32),
            vmem((NF, BLOCKS, LANES), BF16),
            vmem((NX, 1, LANES), F32),
            vmem((NX, 1, LANES), F32),
            vmem((1, LANES), F32),
            vmem((NZ, 1, LANES), F32),
            vmem((NZ, 2 * OWNED, HALF), F32),
            vmem((NZ, 2 * OWNED, HALF), F32),
            vmem((NZ, 2 * OWNED, HALF), BF16),
            vmem((NZ, 2 * OWNED, HALF), BF16),
            vmem((NZ, 2 * OWNED, HALF), BF16),
            vmem((NZ, 2 * OWNED, HALF), BF16),
            vmem((NZ, OWNED, HALF), BF16),
            vmem((NZ, OWNED, HALF), BF16),
            vmem((NZ, OWNED, HALF), BF16),
            vmem((NZ, OWNED, HALF), BF16),
            vmem((NZ, OWNED, COLS), BF16),
            vmem((NZ, OWNED, COLS), BF16),
            dma((6,)),
            dma((2, NZ)),
            dma((2, NX)),
            dma((2, NF)),
            dma((2, NX)),
            dma((2, NZ)),
            dma((2, 2 * NZ)),
            dma((2, 2 * NZ)),
            dma((2, NZ)),
        ],
        compiler_params=pltpu.CompilerParams(collective_id=0, has_side_effects=True),
        name="newton_sketch",
    )(
        pooled,
        labels.reshape(BLOCKS, LANES),
        sign_bits.reshape(BLOCKS, LANES),
        margins_old.reshape(BLOCKS, LANES),
        direction.reshape(1, 16),
        sample_rows.reshape(SAMPLES // LANES, LANES),
    )
    return margins.reshape(ROWS), grad[0, :16], sketch


def solution(mesh):
    return jax.shard_map(
        on_device,
        mesh=mesh,
        in_specs=(P("ex", "feat"), P("ex"), P("ex"), P("ex"), P(("feat", "ex")), P()),
        out_specs=(P("ex"), P(("feat", "ex")), P("ex", "feat")),
        check_vma=False,
    )
```

time: 115 us -> 52.2 us (0.45)
  the two profiles are of different devices: /device:TPU:1 before, /device:TPU:2 now
where the time goes in v1:
time: 52.2 us; the launch traced here: 52 us
  Pallas kernels  47.4 us (91%)
  local copies, waits for them, and re-layouts  3.88 us (7%)
  between operations  0.64 us (1%)
    pallas_call x1, Pallas kernels, on_device(): pl.pallas_call(kernel, out_shape=(jax.ShapeDtypeStruct((BLOCKS, LANES), F...  47.4 us
    unnamed x2, local copies, waits for them, and re-layouts  2.77 us
    squeeze x1, local copies, waits for them, and re-layouts, on_device(): return (margins.reshape(ROWS), grad[0, :16], sketch)  1.11 us

profile of v1, /device:TPU:2, one launch (start us, length us, event | category | flops | bytes accessed | tf_op | source)
XLA Modules:
  0.0 52.0 jit_solution(6121572462075013714)
XLA Ops:
  0.6 47.4 %newton_sketch.1 = (f32[16,128]{1,0:T(8,128)}, f32[1,128]{1,0:T(1,128)}, f32[32,512]{1,0:T(8,128)}) custom-call(bf16[2048,512]{1,0:T(8,128)(2,1)} %pooled_hbm.1, s32[16,128]{1,0:T(8,128)} %bitcast.8, s32[16,128]{1,0:T(8,128)} %bitcast.9, f32[16,128]{1,0:T(8,128)} %bitcast.10, f32[1,16]{1,0:T(1,128)} %bitcast.13, s32[8,128]{1,0:T(8,128)} %bitcast.12), custom_call_target="tpu_custom_call" | custom-call | tf_op jit(solution)/shard_map/newton_sketch/pallas_call | solution.py:259
  48.1 1.1 %slice_bitcast_fusion = f32[16]{0:T(128)} fusion(f32[1,128]{1,0:T(1,128)} %get-tuple-element.7), kind=kLoop, calls=%fused_computation | loop fusion | bytes 128 | tf_op jit(solution)/shard_map/squeeze | solution.py:317
  49.2 1.3 %copy.11 = f32[2048]{0:T(1024)} copy(f32[2048]{0:T(1024)} %bitcast.11) | data formatting | bytes 16384
  50.5 1.5 %copy.12 = f32[32,512]{1,0:T(8,128)} copy(f32[32,512]{1,0:T(8,128)} %get-tuple-element.14) | data formatting | bytes 131072

commit v2 on v1

v2 whole, which is shorter than its diff:
```python
import jax
import jax.numpy as jnp
from jax import lax
from jax.experimental import pallas as pl
from jax.experimental.pallas import tpu as pltpu
from jax.sharding import PartitionSpec as P

NX, NZ, NF = 4, 8, 16
ROWS, COLS, SAMPLES, LANES = 2048, 512, 1024, 128
HALF = COLS // 2
BLOCKS = ROWS // LANES
OWNED = SAMPLES // (NX * NZ)
QUARTER = LANES
F32, BF16 = jnp.float32, jnp.bfloat16
MESH = pl.DeviceIdType.MESH


def parity_sign(ids, mask):
    return 1 - 2 * jnp.bitwise_and(lax.population_count(jnp.bitwise_and(ids, mask)), 1)


FAR_FIRST = (4, 3, 5, 2, 6, 1, 7)


def kernel(
    pooled_hbm, labels_hbm, bits_hbm, old_hbm, dir_hbm, rows_hbm,
    margins_out, grad_out, sketch_out,
    pooled, labels, bits, old, own_dir, rows,
    ids, table, weighted, zdir, xdir, terms,
    xgrad_send, xgrad, zgrad_send, zgrad,
    keep_a, keep_b, keep_c, keep_d, pair_send, pair_got,
    first_send, first_got, second_send, second_got, wide_send, wide_got, slim_send, slim_got,
    in_sem, zdir_sem, xdir_sem, terms_sem, xgrad_sem, zgrad_sem,
    pair_sem, first_sem, second_sem, wide_sem, slim_sem,
):
    ex = lax.axis_index("ex")
    feat = lax.axis_index("feat")
    x, z = ex // NZ, ex % NZ
    flip = x + 1 - 2 * (x % 2)
    back = NX - 1 - x
    across = (x + 2) % NX
    away = 2 * (z % 2) - 1

    def at_x(other):
        return {"ex": other * NZ + z}

    def at_z(step):
        return {"ex": x * NZ + (z + step + 2 * NZ) % NZ}

    def at_feat(step, other):
        return {"feat": (feat // 2 + step) % NZ * 2 + (feat % 2 + other) % 2}

    near = [(step, other) for step in FAR_FIRST for other in range(2)] + [(0, 1)]
    loads = [
        pltpu.make_async_copy(src, dst, in_sem.at[i])
        for i, (src, dst) in enumerate(
            ((dir_hbm, own_dir), (rows_hbm, rows), (pooled_hbm, pooled), (old_hbm, old), (labels_hbm, labels), (bits_hbm, bits))
        )
    ]
    loads[0].start()
    barrier = pltpu.get_barrier_semaphore()
    for step in FAR_FIRST:
        pl.semaphore_signal(barrier, inc=1, device_id=at_z(step), device_id_type=MESH)
    for step in (2, 1, 3):
        pl.semaphore_signal(barrier, inc=1, device_id=at_x((x + step) % NX), device_id_type=MESH)
    for step, other in near:
        pl.semaphore_signal(barrier, inc=1, device_id=at_feat(step, other), device_id_type=MESH)
    for load in loads[1:]:
        load.start()

    def send(src, dst, sems, device, group=0):
        pltpu.make_async_remote_copy(
            src_ref=src, dst_ref=dst, send_sem=sems.at[0], recv_sem=sems.at[1 + group], device_id=device, device_id_type=MESH
        ).start()

    def landed(ref, sems, group=0):
        pltpu.make_async_copy(ref, ref, sems.at[1 + group]).wait()

    def left(ref, sems):
        pltpu.make_async_copy(ref, ref, sems.at[0]).wait()

    loads[0].wait()
    lane_row = lax.broadcasted_iota(jnp.int32, (1, LANES), 1)
    spread = jnp.concatenate([own_dir[...]] * NZ, axis=1)
    zdir[0] = jnp.where(lane_row // 16 == z, spread, 0.0)
    pl.semaphore_wait(barrier, NX + NZ + NF - 3)
    for step in FAR_FIRST:
        send(zdir.at[0], zdir.at[step], zdir_sem, at_z(step))
    loads[1].wait()
    turned = jnp.transpose(rows[...])
    for t in range(SAMPLES // LANES):
        ids[t * LANES : (t + 1) * LANES, :] = jnp.broadcast_to(turned[:, t : t + 1], (LANES, LANES))

    def table_block(index):
        part, step = index // NZ, index % NZ
        offset = away * jnp.where(step % 2 == 1, (NZ - 1 - step) // 2, -((NZ - step) // 2))
        owner = jnp.where(part == 0, x, jnp.where(part == 1, flip, jnp.where(part == 2, back, across)))
        start = pl.multiple_of(owner * (NZ * OWNED) + (z + offset + NZ) % NZ * OWNED, OWNED)
        there = pl.multiple_of(step * (NX * OWNED) + part * OWNED, OWNED)
        wanted = ids[pl.ds(start, OWNED), :]
        lanes = lax.broadcasted_iota(jnp.int32, (OWNED, LANES), 1)
        signs = [None] * BLOCKS
        signs[0] = parity_sign(wanted, ex * ROWS + lanes).astype(F32).astype(BF16)
        for bit in range(4):
            this = (1 - 2 * jnp.bitwise_and(jnp.right_shift(wanted, 7 + bit), 1)).astype(F32).astype(BF16)
            for low in range(1 << bit):
                signs[low + (1 << bit)] = signs[low] * this
        for block in range(BLOCKS):
            table[pl.ds(there, OWNED), block * LANES : (block + 1) * LANES] = signs[block]

    pl.loop(0, 20)(table_block)
    landed(zdir.at[1:], zdir_sem)
    row = zdir[0]
    for step in range(1, NZ):
        row = row + zdir[step]
    xdir[x] = row
    for step in (2, 1, 3):
        send(xdir.at[x], xdir.at[x], xdir_sem, at_x((x + step) % NX))
    pl.loop(20, 32)(table_block)
    loads[2].wait()
    landed(xdir.at[1:], xdir_sem)
    step_dir = jnp.concatenate([xdir[i] for i in range(NX)], axis=1).astype(BF16)
    step_dir = jnp.broadcast_to(step_dir, (BLOCKS, COLS))
    block_row = lax.broadcasted_iota(jnp.int32, (BLOCKS, LANES), 0)
    partial = jnp.zeros((BLOCKS, LANES), F32)
    for block in range(BLOCKS):
        here = lax.dot_general(
            step_dir,
            pooled[block * LANES : (block + 1) * LANES, :],
            (((1,), (1,)), ((), ())),
            preferred_element_type=F32,
        )
        partial = jnp.where(block_row == block, here, partial)
    terms[feat] = partial.astype(BF16)
    for step, other in near:
        send(terms.at[feat], terms.at[feat], terms_sem, at_feat(step, other))
    for load in loads[3:]:
        load.wait()
    landed(terms.at[1:], terms_sem)
    total = terms[0].astype(F32)
    for i in range(1, NF):
        total = total + terms[i].astype(F32)
    margins = old[...] + total
    margins_out[...] = margins
    decay = jnp.exp(-jnp.abs(margins))
    likely = 1.0 / (1.0 + decay)
    rare = decay * likely
    weight = jnp.sqrt(likely * rare)
    residual = jnp.where(margins >= 0, likely, rare) - labels[...].astype(F32)
    scale = (2 * bits[...] - 1).astype(F32) * weight
    columns = jnp.transpose(scale)
    for block in range(BLOCKS):
        at = slice(block * LANES, (block + 1) * LANES)
        weighted[at, :] = (pooled[at, :].astype(F32) * columns[:, block : block + 1]).astype(BF16)

    def launch_first(i):
        send(first_send.at[2 * i], first_got.at[2 * i], first_sem, at_x(flip), i)
        send(first_send.at[2 * i + 1], first_got.at[2 * i + 1], first_sem, at_x(back), i)

    def compute(pair):
        at = slice(pair * 2 * NX * OWNED, (pair + 1) * 2 * NX * OWNED)
        product = [
            jnp.dot(table[at, :], weighted[:, i * HALF : (i + 1) * HALF], preferred_element_type=F32) for i in range(2)
        ]
        sends = []
        for k in range(2):
            i = 2 * pair + k
            block = product[1][k * NX * OWNED : (k + 1) * NX * OWNED]
            for colour, keeps, keep, device in ((0, (1, 3, 5, 7), keep_c, at_z(-away)), (1, (2, 4, 6, 7), keep_d, at_z(away))):
                part = block[:, colour * QUARTER : (colour + 1) * QUARTER]
                if i in keeps:
                    keep[keeps.index(i)] = part
                else:
                    n = [j for j in range(NZ) if j not in keeps].index(i)
                    slot = 2 * n + colour
                    pair_send[slot] = part.astype(BF16)
                    sends.append((slot, n, device))
            block = product[0][k * NX * OWNED : (k + 1) * NX * OWNED]
            g = [slice(j * OWNED, (j + 1) * OWNED) for j in range(NX)]
            keep_a[i, :OWNED, :] = block[g[0], :QUARTER]
            keep_a[i, OWNED:, :] = block[g[2], :QUARTER]
            first_send[2 * i, :OWNED, :] = block[g[1], :QUARTER].astype(BF16)
            first_send[2 * i, OWNED:, :] = block[g[3], :QUARTER].astype(BF16)
            keep_b[i] = block[: 2 * OWNED, QUARTER:]
            first_send[2 * i + 1] = block[2 * OWNED :, QUARTER:].astype(BF16)
        for slot, n, device in sends:
            send(pair_send.at[slot], pair_got.at[slot], pair_sem, device, n)
        launch_first(2 * pair)
        launch_first(2 * pair + 1)

    def after_pair(n):
        landed(pair_got.at[2 * n : 2 * n + 2], pair_sem, n)
        i = NZ + n
        c, d = 2 * n, 2 * n + 1
        first_send[2 * i, :OWNED, :] = (keep_c[n, OWNED : 2 * OWNED, :] + pair_got[c, OWNED : 2 * OWNED, :].astype(F32)).astype(BF16)
        first_send[2 * i, OWNED:, :] = (keep_c[n, 3 * OWNED :, :] + pair_got[c, 3 * OWNED :, :].astype(F32)).astype(BF16)
        first_send[2 * i + 1] = (keep_d[n, 2 * OWNED :, :] + pair_got[d, 2 * OWNED :, :].astype(F32)).astype(BF16)
        launch_first(i)
        keep_a[i, :OWNED, :] = keep_c[n, :OWNED, :] + pair_got[c, :OWNED, :].astype(F32)
        keep_a[i, OWNED:, :] = keep_c[n, 2 * OWNED : 3 * OWNED, :] + pair_got[c, 2 * OWNED : 3 * OWNED, :].astype(F32)
        keep_b[i] = keep_d[n, : 2 * OWNED, :] + pair_got[d, : 2 * OWNED, :].astype(F32)

    def after_first(i):
        landed(first_got.at[2 * i : 2 * i + 2], first_sem, i)
        second_send[2 * i] = (keep_a[i, OWNED:, :] + first_got[2 * i, OWNED:, :].astype(F32)).astype(BF16)
        second_send[2 * i + 1] = (keep_b[i, OWNED:, :] + first_got[2 * i + 1, OWNED:, :].astype(F32)).astype(BF16)
        send(second_send.at[2 * i], second_got.at[2 * i], second_sem, at_x(back), i)
        send(second_send.at[2 * i + 1], second_got.at[2 * i + 1], second_sem, at_x(flip), i)

    def after_second(i):
        landed(second_got.at[2 * i : 2 * i + 2], second_sem, i)
        return (
            keep_a[i, :OWNED, :] + first_got[2 * i, :OWNED, :].astype(F32) + second_got[2 * i].astype(F32),
            keep_b[i, :OWNED, :] + first_got[2 * i + 1, :OWNED, :].astype(F32) + second_got[2 * i + 1].astype(F32),
        )

    def wide(i):
        sum_a, sum_b = after_second(i)
        wide_send[i, :, :QUARTER] = sum_a.astype(BF16)
        wide_send[i, :, QUARTER:] = sum_b.astype(BF16)
        offset = (NZ - 1 - i) // 2 if i % 2 else -((NZ - i) // 2)
        send(wide_send.at[i], wide_got.at[i], wide_sem, at_z(away * offset))

    def slim(n):
        sum_c, sum_d = after_second(NZ + n)
        slim_send[2 * n] = sum_c.astype(BF16)
        slim_send[2 * n + 1] = sum_d.astype(BF16)
        send(slim_send.at[2 * n], slim_got.at[2 * n], slim_sem, at_z(away * (NX - 1 - n)))
        send(slim_send.at[2 * n + 1], slim_got.at[2 * n + 1], slim_sem, at_z(-away * (NX - 1 - n)))

    compute(0)
    compute(1)
    compute(2)
    compute(3)
    flat = jnp.concatenate([residual[i : i + 1, :] for i in range(BLOCKS)], axis=1).astype(BF16)
    grad = jnp.dot(jnp.broadcast_to(flat, (8, ROWS)), pooled[...], preferred_element_type=F32)[0:1, :]
    for i in range(NX):
        xgrad_send[i] = grad[:, i * LANES : (i + 1) * LANES]
    for step in (2, 1, 3):
        send(xgrad_send.at[(x + step) % NX], xgrad.at[step], xgrad_sem, at_x((x + step) % NX))
    after_pair(0)
    after_first(0)
    after_first(1)
    after_pair(1)
    after_first(2)
    after_first(3)
    after_pair(2)
    after_first(4)
    after_first(5)
    after_pair(3)
    after_first(8)
    wide(0)
    after_first(6)
    after_first(7)
    wide(1)
    wide(2)
    after_first(9)
    wide(3)
    wide(4)
    landed(xgrad.at[1:], xgrad_sem)
    part = xgrad_send[x]
    for step in range(1, NX):
        part = part + xgrad[step]
    zgrad_send[...] = part
    for step in FAR_FIRST:
        send(zgrad_send, zgrad.at[step], zgrad_sem, at_z(step))
    after_first(10)
    slim(0)
    wide(5)
    wide(6)
    after_first(11)
    slim(1)
    slim(2)
    sum_a, sum_b = after_second(NZ - 1)
    sum_c, sum_d = after_second(NZ + NX - 1)
    landed(zgrad.at[1:], zgrad_sem)
    part = zgrad_send[...]
    for step in range(1, NZ):
        part = part + zgrad[step]
    grad_out[...] = pltpu.roll(part, (NZ - z) * 16 % LANES, 1)[:, :16] * (1.0 / 256.0)
    landed(wide_got, wide_sem)
    for i in range(NZ - 1):
        sum_a = sum_a + wide_got[i, :, :QUARTER].astype(F32)
        sum_b = sum_b + wide_got[i, :, QUARTER:].astype(F32)
    landed(slim_got, slim_sem)
    for n in range(NX - 1):
        sum_c = sum_c + slim_got[2 * n].astype(F32)
        sum_d = sum_d + slim_got[2 * n + 1].astype(F32)
    for i, part in enumerate((sum_a, sum_b, sum_c, sum_d)):
        sketch_out[:, i * QUARTER : (i + 1) * QUARTER] = part * (1.0 / 32.0)
    left(zdir.at[1:], zdir_sem)
    left(xdir.at[1:], xdir_sem)
    left(terms.at[1:], terms_sem)
    left(xgrad.at[1:], xgrad_sem)
    left(zgrad.at[1:], zgrad_sem)
    left(pair_send, pair_sem)
    left(first_send, first_sem)
    left(second_send, second_sem)
    left(wide_send, wide_sem)
    left(slim_send, slim_sem)


def put_out(margins, grad, sketch, margins_hbm, grad_hbm, sketch_hbm, sem):
    copies = [
        pltpu.make_async_copy(src, dst, sem.at[i])
        for i, (src, dst) in enumerate(((sketch, sketch_hbm), (margins, margins_hbm), (grad, grad_hbm)))
    ]
    for copy in copies:
        copy.start()
    for copy in copies:
        copy.wait()


def on_device(pooled, labels, sign_bits, margins_old, direction, sample_rows):
    dma = pltpu.SemaphoreType.DMA
    vmem = pltpu.VMEM
    margins, grad, sketch = pl.pallas_call(
        kernel,
        out_shape=(
            jax.ShapeDtypeStruct((BLOCKS, LANES), F32),
            jax.ShapeDtypeStruct((1, 16), F32),
            jax.ShapeDtypeStruct((OWNED, COLS), F32),
        ),
        in_specs=[pl.BlockSpec(memory_space=pl.ANY)] * 6,
        out_specs=[pl.BlockSpec(memory_space=vmem)] * 3,
        scratch_shapes=[
            vmem((ROWS, COLS), BF16),
            vmem((BLOCKS, LANES), jnp.int32),
            vmem((BLOCKS, LANES), jnp.int32),
            vmem((BLOCKS, LANES), F32),
            vmem((1, 16), F32),
            vmem((SAMPLES // LANES, LANES), jnp.int32),
            vmem((SAMPLES, LANES), jnp.int32),
            vmem((SAMPLES, ROWS), BF16),
            vmem((ROWS, COLS), BF16),
            vmem((NZ, 1, LANES), F32),
            vmem((NX, 1, LANES), F32),
            vmem((NF, BLOCKS, LANES), BF16),
            vmem((NX, 1, LANES), F32),
            vmem((NX, 1, LANES), F32),
            vmem((1, LANES), F32),
            vmem((NZ, 1, LANES), F32),
            vmem((NZ + NX, 2 * OWNED, QUARTER), F32),
            vmem((NZ + NX, 2 * OWNED, QUARTER), F32),
            vmem((NX, NX * OWNED, QUARTER), F32),
            vmem((NX, NX * OWNED, QUARTER), F32),
            vmem((2 * NX, NX * OWNED, QUARTER), BF16),
            vmem((2 * NX, NX * OWNED, QUARTER), BF16),
            vmem((2 * (NZ + NX), 2 * OWNED, QUARTER), BF16),
            vmem((2 * (NZ + NX), 2 * OWNED, QUARTER), BF16),
            vmem((2 * (NZ + NX), OWNED, QUARTER), BF16),
            vmem((2 * (NZ + NX), OWNED, QUARTER), BF16),
            vmem((NZ - 1, OWNED, 2 * QUARTER), BF16),
            vmem((NZ - 1, OWNED, 2 * QUARTER), BF16),
            vmem((2 * (NX - 1), OWNED, QUARTER), BF16),
            vmem((2 * (NX - 1), OWNED, QUARTER), BF16),
            dma((6,)),
            dma((2,)),
            dma((2,)),
            dma((2,)),
            dma((2,)),
            dma((2,)),
            dma((1 + NX,)),
            dma((1 + NZ + NX,)),
            dma((1 + NZ + NX,)),
            dma((2,)),
            dma((2,)),
        ],
        compiler_params=pltpu.CompilerParams(vmem_limit_bytes=40 << 20, collective_id=0, has_side_effects=True),
        name="newton_sketch",
    )(*(pltpu.with_memory_space_constraint(array, pltpu.HBM) for array in (
        pooled,
        labels.reshape(BLOCKS, LANES),
        sign_bits.reshape(BLOCKS, LANES),
        margins_old.reshape(BLOCKS, LANES),
        direction.reshape(1, 16),
        sample_rows.reshape(SAMPLES // LANES, LANES),
    )))
    margins, grad, sketch = pl.pallas_call(
        put_out,
        out_shape=(
            jax.ShapeDtypeStruct((BLOCKS, LANES), F32),
            jax.ShapeDtypeStruct((1, 16), F32),
            jax.ShapeDtypeStruct((OWNED, COLS), F32),
        ),
        in_specs=[pl.BlockSpec(memory_space=vmem)] * 3,
        out_specs=[pl.BlockSpec(memory_space=pl.ANY)] * 3,
        scratch_shapes=[dma((3,))],
        compiler_params=pltpu.CompilerParams(vmem_limit_bytes=1 << 20),
        name="put_out",
    )(margins, grad, sketch)
    return margins.reshape(ROWS), grad.reshape(16), sketch


def solution(mesh):
    return jax.shard_map(
        on_device,
        mesh=mesh,
        in_specs=(P("ex", "feat"), P("ex"), P("ex"), P("ex"), P(("feat", "ex")), P()),
        out_specs=(P("ex"), P(("feat", "ex")), P("ex", "feat")),
        check_vma=False,
    )
```

time: 52.2 us -> 44.9 us (0.86)
  the two profiles are of different devices: /device:TPU:2 before, /device:TPU:1 now
where the time goes in v2:
time: 44.9 us; the launch traced here: 44.8 us
  Pallas kernels  44.1 us (98%)
  between operations  0.64 us (1%)
    pallas_call x1, Pallas kernels, on_device(): pl.pallas_call(kernel, out_shape=(jax.ShapeDtypeStruct((BLOCKS, LANES), F...  43.5 us

profile of v2, /device:TPU:1, one launch (start us, length us, event | category | flops | bytes accessed | tf_op | source)
XLA Modules:
  0.0 44.8 jit_solution(8841919078447447267)
XLA Ops:
  0.6 43.5 %newton_sketch.1 = (f32[16,128]{1,0:T(8,128)S(1)}, f32[1,16]{1,0:T(1,128)S(1)}, f32[32,512]{1,0:T(8,128)S(1)}) custom-call(bf16[2048,512]{1,0:T(8,128)(2,1)} %pooled_hbm.1, s32[16,128]{1,0:T(8,128)} %bitcast.7, s32[16,128]{1,0:T(8,128)} %bitcast.8, f32[16,128]{1,0:T(8,128)} %bitcast.9, f32[1,16]{1,0:T(1,128)} %bitcast.11, s32[8,128]{1,0:T(8,128)} %bitcast.10), custom_call_target="tpu_custom_call" | custom-call | tf_op jit(solution)/shard_map/newton_sketch/pallas_call | solution.py:317
  44.1 0.7 %put_out.1 = (f32[16,128]{1,0:T(8,128)}, f32[1,16]{1,0:T(1,128)}, f32[32,512]{1,0:T(8,128)}) custom-call(f32[16,128]{1,0:T(8,128)S(1)} %get-tuple-element.9.margins, f32[1,16]{1,0:T(1,128)S(1)} %get-tuple-element.10.grad, f32[32,512]{1,0:T(8,128)S(1)} %get-tuple-element.11.sketch), custom_call_target="tpu_custom_call" | custom-call | tf_op jit(solution)/shard_map/put_out/pallas_call | solution.py:379

commit v3 on v2

--- a/solution.py
+++ b/solution.py
@@ -20,6 +20,7 @@
 
 
 FAR_FIRST = (4, 3, 5, 2, 6, 1, 7)
+DIRECT = (0, 1, 2, 7)
 
 
 def kernel(
@@ -30,8 +31,9 @@
     xgrad_send, xgrad, zgrad_send, zgrad,
     keep_a, keep_b, keep_c, keep_d, pair_send, pair_got,
     first_send, first_got, second_send, second_got, wide_send, wide_got, slim_send, slim_got,
+    keep_w, direct_send, direct_got,
     in_sem, zdir_sem, xdir_sem, terms_sem, xgrad_sem, zgrad_sem,
-    pair_sem, first_sem, second_sem, wide_sem, slim_sem,
+    pair_sem, first_sem, second_sem, wide_sem, slim_sem, direct_sem,
 ):
     ex = lax.axis_index("ex")
     feat = lax.axis_index("feat")
@@ -115,22 +117,34 @@
         row = row + zdir[step]
     xdir[x] = row
     for step in (2, 1, 3):
-        send(xdir.at[x], xdir.at[x], xdir_sem, at_x((x + step) % NX))
+        send(xdir.at[x], xdir.at[x], xdir_sem, at_x((x + step) % NX), step - 1)
+
+    block_row = lax.broadcasted_iota(jnp.int32, (BLOCKS, LANES), 0)
+
+    def product_of(other):
+        part = jnp.broadcast_to(xdir[other], (BLOCKS, LANES)).astype(BF16)
+        features = pl.ds(pl.multiple_of(other * LANES, LANES), LANES)
+        result = jnp.zeros((BLOCKS, LANES), F32)
+        for pair in range(BLOCKS // 2):
+            here = lax.dot_general(
+                part,
+                pooled[pair * 2 * LANES : (pair + 1) * 2 * LANES, features],
+                (((1,), (1,)), ((), ())),
+                preferred_element_type=F32,
+            )
+            result = jnp.where(block_row == 2 * pair, here[:, :LANES], result)
+            result = jnp.where(block_row == 2 * pair + 1, here[:, LANES:], result)
+        return result
+
     pl.loop(20, 32)(table_block)
     loads[2].wait()
-    landed(xdir.at[1:], xdir_sem)
-    step_dir = jnp.concatenate([xdir[i] for i in range(NX)], axis=1).astype(BF16)
-    step_dir = jnp.broadcast_to(step_dir, (BLOCKS, COLS))
-    block_row = lax.broadcasted_iota(jnp.int32, (BLOCKS, LANES), 0)
-    partial = jnp.zeros((BLOCKS, LANES), F32)
-    for block in range(BLOCKS):
-        here = lax.dot_general(
-            step_dir,
-            pooled[block * LANES : (block + 1) * LANES, :],
-            (((1,), (1,)), ((), ())),
-            preferred_element_type=F32,
-        )
-        partial = jnp.where(block_row == block, here, partial)
+    partial = product_of(x)
+    landed(xdir.at[0], xdir_sem, 0)
+    partial = partial + product_of((x + NX - 1) % NX)
+    landed(xdir.at[0], xdir_sem, 2)
+    partial = partial + product_of((x + NX - 3) % NX)
+    landed(xdir.at[0], xdir_sem, 1)
+    partial = partial + product_of((x + NX - 2) % NX)
     terms[feat] = partial.astype(BF16)
     for step, other in near:
         send(terms.at[feat], terms.at[feat], terms_sem, at_feat(step, other))
@@ -157,14 +171,13 @@
         send(first_send.at[2 * i], first_got.at[2 * i], first_sem, at_x(flip), i)
         send(first_send.at[2 * i + 1], first_got.at[2 * i + 1], first_sem, at_x(back), i)
 
-    def compute(pair):
-        at = slice(pair * 2 * NX * OWNED, (pair + 1) * 2 * NX * OWNED)
+    def compute(*blocks):
+        at = slice(blocks[0] * NX * OWNED, (blocks[-1] + 1) * NX * OWNED)
         product = [
             jnp.dot(table[at, :], weighted[:, i * HALF : (i + 1) * HALF], preferred_element_type=F32) for i in range(2)
         ]
         sends = []
-        for k in range(2):
-            i = 2 * pair + k
+        for k, i in enumerate(blocks):
             block = product[1][k * NX * OWNED : (k + 1) * NX * OWNED]
             for colour, keeps, keep, device in ((0, (1, 3, 5, 7), keep_c, at_z(-away)), (1, (2, 4, 6, 7), keep_d, at_z(away))):
                 part = block[:, colour * QUARTER : (colour + 1) * QUARTER]
@@ -177,6 +190,13 @@
                     sends.append((slot, n, device))
             block = product[0][k * NX * OWNED : (k + 1) * NX * OWNED]
             g = [slice(j * OWNED, (j + 1) * OWNED) for j in range(NX)]
+            if i in DIRECT:
+                n = DIRECT.index(i)
+                keep_w[n] = block[g[0]]
+                direct_send[3 * n] = block[g[1]].astype(BF16)
+                direct_send[3 * n + 1] = block[g[2]].astype(BF16)
+                direct_send[3 * n + 2] = block[g[3]].astype(BF16)
+                continue
             keep_a[i, :OWNED, :] = block[g[0], :QUARTER]
             keep_a[i, OWNED:, :] = block[g[2], :QUARTER]
             first_send[2 * i, :OWNED, :] = block[g[1], :QUARTER].astype(BF16)
@@ -185,8 +205,22 @@
             first_send[2 * i + 1] = block[2 * OWNED :, QUARTER:].astype(BF16)
         for slot, n, device in sends:
             send(pair_send.at[slot], pair_got.at[slot], pair_sem, device, n)
-        launch_first(2 * pair)
-        launch_first(2 * pair + 1)
+
+    def launch_x(i):
+        if i not in DIRECT:
+            launch_first(i)
+            return
+        n = DIRECT.index(i)
+        for j, other in ((2, across), (0, flip), (1, back)):
+            send(direct_send.at[3 * n + j], direct_got.at[3 * n + j], direct_sem, at_x(other), n)
+
+    def after_direct(i):
+        n = DIRECT.index(i)
+        landed(direct_got.at[3 * n : 3 * n + 3], direct_sem, n)
+        result = keep_w[n]
+        for j in range(3):
+            result = result + direct_got[3 * n + j].astype(F32)
+        return result[:, :QUARTER], result[:, QUARTER:]
 
     def after_pair(n):
         landed(pair_got.at[2 * n : 2 * n + 2], pair_sem, n)
@@ -215,23 +249,39 @@
         )
 
     def wide(i):
-        sum_a, sum_b = after_second(i)
+        sum_a, sum_b = after_direct(i) if i in DIRECT else after_second(i)
         wide_send[i, :, :QUARTER] = sum_a.astype(BF16)
         wide_send[i, :, QUARTER:] = sum_b.astype(BF16)
         offset = (NZ - 1 - i) // 2 if i % 2 else -((NZ - i) // 2)
         send(wide_send.at[i], wide_got.at[i], wide_sem, at_z(away * offset))
 
+    def at_far(other, step):
+        return {"ex": other * NZ + (z + step + 2 * NZ) % NZ}
+
     def slim(n):
-        sum_c, sum_d = after_second(NZ + n)
-        slim_send[2 * n] = sum_c.astype(BF16)
-        slim_send[2 * n + 1] = sum_d.astype(BF16)
-        send(slim_send.at[2 * n], slim_got.at[2 * n], slim_sem, at_z(away * (NX - 1 - n)))
-        send(slim_send.at[2 * n + 1], slim_got.at[2 * n + 1], slim_sem, at_z(-away * (NX - 1 - n)))
+        i = NZ + n
+        landed(first_got.at[2 * i : 2 * i + 2], first_sem, i)
+        sum_c = keep_a[i] + first_got[2 * i].astype(F32)
+        sum_d = keep_b[i] + first_got[2 * i + 1].astype(F32)
+        ahead = away * (NX - 1 - n)
+        routes = [(sum_c[OWNED:], back, ahead), (sum_d[OWNED:], flip, -ahead), (sum_c[:OWNED], x, ahead), (sum_d[:OWNED], x, -ahead)]
+        for j, (part, other, step) in enumerate(routes[: 2 if n == NX - 1 else 4]):
+            slim_send[4 * n + j] = part.astype(BF16)
+            send(slim_send.at[4 * n + j], slim_got.at[4 * n + j], slim_sem, at_far(other, step))
+        return sum_c[:OWNED], sum_d[:OWNED]
 
     compute(0)
-    compute(1)
-    compute(2)
-    compute(3)
+    launch_x(0)
+    compute(1, 2)
+    launch_x(1)
+    launch_x(2)
+    compute(3, 4)
+    launch_x(3)
+    launch_x(4)
+    compute(5, 6)
+    launch_x(5)
+    launch_x(6)
+    compute(7)
     flat = jnp.concatenate([residual[i : i + 1, :] for i in range(BLOCKS)], axis=1).astype(BF16)
     grad = jnp.dot(jnp.broadcast_to(flat, (8, ROWS)), pooled[...], preferred_element_type=F32)[0:1, :]
     for i in range(NX):
@@ -239,24 +289,18 @@
     for step in (2, 1, 3):
         send(xgrad_send.at[(x + step) % NX], xgrad.at[step], xgrad_sem, at_x((x + step) % NX))
     after_pair(0)
-    after_first(0)
-    after_first(1)
+    wide(0)
     after_pair(1)
-    after_first(2)
+    wide(1)
     after_first(3)
     after_pair(2)
     after_first(4)
     after_first(5)
+    wide(2)
     after_pair(3)
-    after_first(8)
-    wide(0)
+    launch_x(7)
     after_first(6)
-    after_first(7)
-    wide(1)
-    wide(2)
-    after_first(9)
-    wide(3)
-    wide(4)
+    slim(0)
     landed(xgrad.at[1:], xgrad_sem)
     part = xgrad_send[x]
     for step in range(1, NX):
@@ -264,15 +308,14 @@
     zgrad_send[...] = part
     for step in FAR_FIRST:
         send(zgrad_send, zgrad.at[step], zgrad_sem, at_z(step))
-    after_first(10)
-    slim(0)
+    wide(3)
+    slim(1)
+    wide(4)
+    slim(2)
     wide(5)
+    sum_c, sum_d = slim(3)
     wide(6)
-    after_first(11)
-    slim(1)
-    slim(2)
-    sum_a, sum_b = after_second(NZ - 1)
-    sum_c, sum_d = after_second(NZ + NX - 1)
+    sum_a, sum_b = after_direct(NZ - 1)
     landed(zgrad.at[1:], zgrad_sem)
     part = zgrad_send[...]
     for step in range(1, NZ):
@@ -283,9 +326,9 @@
         sum_a = sum_a + wide_got[i, :, :QUARTER].astype(F32)
         sum_b = sum_b + wide_got[i, :, QUARTER:].astype(F32)
     landed(slim_got, slim_sem)
-    for n in range(NX - 1):
-        sum_c = sum_c + slim_got[2 * n].astype(F32)
-        sum_d = sum_d + slim_got[2 * n + 1].astype(F32)
+    for slot in range(0, 4 * NX - 2, 2):
+        sum_c = sum_c + slim_got[slot].astype(F32)
+        sum_d = sum_d + slim_got[slot + 1].astype(F32)
     for i, part in enumerate((sum_a, sum_b, sum_c, sum_d)):
         sketch_out[:, i * QUARTER : (i + 1) * QUARTER] = part * (1.0 / 32.0)
     left(zdir.at[1:], zdir_sem)
@@ -294,8 +337,9 @@
     left(xgrad.at[1:], xgrad_sem)
     left(zgrad.at[1:], zgrad_sem)
     left(pair_send, pair_sem)
-    left(first_send, first_sem)
-    left(second_send, second_sem)
+    left(first_send.at[: 2 * (NX + NZ - len(DIRECT))], first_sem)
+    left(second_send.at[: 2 * (NZ - len(DIRECT))], second_sem)
+    left(direct_send, direct_sem)
     left(wide_send, wide_sem)
     left(slim_send, slim_sem)
 
@@ -348,23 +392,27 @@
             vmem((2 * NX, NX * OWNED, QUARTER), BF16),
             vmem((2 * (NZ + NX), 2 * OWNED, QUARTER), BF16),
             vmem((2 * (NZ + NX), 2 * OWNED, QUARTER), BF16),
-            vmem((2 * (NZ + NX), OWNED, QUARTER), BF16),
-            vmem((2 * (NZ + NX), OWNED, QUARTER), BF16),
+            vmem((2 * NZ, OWNED, QUARTER), BF16),
+            vmem((2 * NZ, OWNED, QUARTER), BF16),
             vmem((NZ - 1, OWNED, 2 * QUARTER), BF16),
             vmem((NZ - 1, OWNED, 2 * QUARTER), BF16),
-            vmem((2 * (NX - 1), OWNED, QUARTER), BF16),
-            vmem((2 * (NX - 1), OWNED, QUARTER), BF16),
+            vmem((4 * NX - 2, OWNED, QUARTER), BF16),
+            vmem((4 * NX - 2, OWNED, QUARTER), BF16),
+            vmem((len(DIRECT), OWNED, HALF), F32),
+            vmem((3 * len(DIRECT), OWNED, HALF), BF16),
+            vmem((3 * len(DIRECT), OWNED, HALF), BF16),
             dma((6,)),
             dma((2,)),
-            dma((2,)),
+            dma((NX,)),
             dma((2,)),
             dma((2,)),
             dma((2,)),
             dma((1 + NX,)),
             dma((1 + NZ + NX,)),
-            dma((1 + NZ + NX,)),
-            dma((2,)),
-            dma((2,)),
+            dma((1 + NZ,)),
+            dma((2,)),
+            dma((2,)),
+            dma((1 + len(DIRECT),)),
         ],
         compiler_params=pltpu.CompilerParams(vmem_limit_bytes=40 << 20, collective_id=0, has_side_effects=True),
         name="newton_sketch",

time: 44.9 us -> 43.8 us (0.976)
  Pallas kernels: 44.1 us -> 43.1 us
    pallas_call x1, Pallas kernels: 43.5 us -> 42.4 us  [on_device(): pl.pallas_call(kernel, out_shape=(jax.ShapeDtypeStruct((BLOCKS, LANES), F...]
where the time goes in v3:
time: 43.8 us; the launch traced here: 43.7 us
  Pallas kernels  43.1 us (98%)
  between operations  0.64 us (1%)
    pallas_call x1, Pallas kernels, on_device(): pl.pallas_call(kernel, out_shape=(jax.ShapeDtypeStruct((BLOCKS, LANES), F...  42.4 us

profile of v3, /device:TPU:1, one launch (start us, length us, event | category | flops | bytes accessed | tf_op | source)
XLA Modules:
  0.0 43.7 jit_solution(102898805924948922)
XLA Ops:
  0.6 42.4 %newton_sketch.1 = (f32[16,128]{1,0:T(8,128)S(1)}, f32[1,16]{1,0:T(1,128)S(1)}, f32[32,512]{1,0:T(8,128)S(1)}) custom-call(bf16[2048,512]{1,0:T(8,128)(2,1)} %pooled_hbm.1, s32[16,128]{1,0:T(8,128)} %bitcast.7, s32[16,128]{1,0:T(8,128)} %bitcast.8, f32[16,128]{1,0:T(8,128)} %bitcast.9, f32[1,16]{1,0:T(1,128)} %bitcast.11, s32[8,128]{1,0:T(8,128)} %bitcast.10), custom_call_target="tpu_custom_call" | custom-call | tf_op jit(solution)/shard_map/newton_sketch/pallas_call | solution.py:361
  43.1 0.7 %put_out.1 = (f32[16,128]{1,0:T(8,128)}, f32[1,16]{1,0:T(1,128)}, f32[32,512]{1,0:T(8,128)}) custom-call(f32[16,128]{1,0:T(8,128)S(1)} %get-tuple-element.9.margins, f32[1,16]{1,0:T(1,128)S(1)} %get-tuple-element.10.grad, f32[32,512]{1,0:T(8,128)S(1)} %get-tuple-element.11.sketch), custom_call_target="tpu_custom_call" | custom-call | tf_op jit(solution)/shard_map/put_out/pallas_call | solution.py:427
